TPU v7x, 32 devices: a whole 2x2x4 slice. The times are simulated.
32 devices in a mesh: expert: 16 (over z, y, x), vocab: 2 (over core).
Axes of the slice: x: 2, y: 2, z: 4, core: 2. Of those that a mesh axis runs over, the one named last changes fastest.
Arguments:
- out_grad: bfloat16 [2048, 4096], P('expert', 'vocab'), may hold values from -6 to 6
- residual_stream: bfloat16 [2048, 4096], P('expert', 'vocab'), may hold values from -228 to 228
- norm_gain: float32 [4096], P('vocab'), may hold values from 0.25 to 51
- expert_ids: int32 [2048, 8], P('expert'), may hold values from 0 to 15, all different within a row; in each aligned block of 128 rows (0 to 127, 128 to 255, ...) at most 76 rows name the same one
- gate_scores: float32 [2048, 8], P('expert'), may hold values from 0.05 to 1
- saved_gate: bfloat16 [16, 1216, 1536], P('expert', None, 'vocab'), may hold values from -6 to 6
- saved_up: bfloat16 [16, 1216, 1536], P('expert', None, 'vocab'), may hold values from -6 to 6
- gate_weight: bfloat16 [16, 4096, 1536], P('expert', None, 'vocab'), may hold values from -0.09375 to 0.09375
- up_weight: bfloat16 [16, 4096, 1536], P('expert', None, 'vocab'), may hold values from -0.09375 to 0.09375
- down_weight: bfloat16 [16, 1536, 4096], P('expert', 'vocab'), may hold values from -0.15625 to 0.15625
- embedding: bfloat16 [12288, 4096], P(('expert', 'vocab')), may hold values from -0.09375 to 0.09375
- allowed: int32 [12288], P(('expert', 'vocab')), may hold values 0 or 1
- suffix_start: int32 [16], P('expert'), may hold values from 0 to 108
Outputs:
- token_grad: bfloat16 [2048, 4096], P('expert', 'vocab')
- scores: float32 [320, 12288], P(None, ('expert', 'vocab'))
Inputs may be any that keep to these rules, and one draw needn't show every extreme that they name: `expert_ids`: in each aligned block of 128 rows (one behavior) a row names 8 different experts and no expert is named by more than 76 rows; some expert is named by exactly 76 rows in some blocks.
All inputs are finite; a program needn't handle non-finite values. No bound on the sum of `allowed` on one device may be relied on, other than what follows from the above.
Results may differ from a plain program's by a relative error of at most 0.01.
Values may be sent and summed in bfloat16 or wider, within the bound.
A program may use at most 128 MiB of HBM per device.

v0:
```python
import jax
import jax.numpy as jnp
from jax import lax
from jax.sharding import PartitionSpec as P

D = 4096
SUFFIX = 20


def shards(
    out_grad,
    residual_stream,
    norm_gain,
    expert_ids,
    gate_scores,
    saved_gate,
    saved_up,
    gate_weight,
    up_weight,
    down_weight,
    embedding,
    allowed,
    suffix_start,
):
    n_expert = lax.axis_size("expert")
    seq_len, d_slice = out_grad.shape
    top_k = expert_ids.shape[1]
    slot_count = saved_gate.shape[1]
    capacity = slot_count // n_expert
    contract = (((1,), (1,)), ((), ()))
    chosen = expert_ids.reshape(-1)
    matches = (chosen[:, None] == jnp.arange(n_expert, dtype=jnp.int32)[None, :]).astype(jnp.int32)
    before = jnp.cumsum(matches, axis=0) - matches
    position = jnp.sum(before * matches, axis=1)
    target = chosen * capacity + position
    gate_share = gate_scores / jnp.sum(gate_scores, axis=1, keepdims=True)
    routed = (gate_share[:, :, None] * out_grad.astype(jnp.float32)[:, None, :]).astype(
        jnp.bfloat16
    )
    routed = routed.reshape(seq_len * top_k, d_slice)
    buffer = jnp.zeros((slot_count, d_slice), jnp.bfloat16).at[target].set(routed)
    arrived = lax.all_to_all(buffer, "expert", split_axis=0, concat_axis=0, tiled=True)
    incoming = lax.all_gather(arrived, "vocab", axis=1, tiled=True)
    act_grad = lax.dot_general(
        incoming, down_weight[0], contract, preferred_element_type=jnp.float32
    )
    pre_gate = saved_gate[0].astype(jnp.float32)
    pre_up = saved_up[0].astype(jnp.float32)
    sigmoid_g = jax.nn.sigmoid(pre_gate)
    gate_grad = (act_grad * pre_up * sigmoid_g * (1.0 + pre_gate * (1.0 - sigmoid_g))).astype(
        jnp.bfloat16
    )
    up_grad = (act_grad * pre_gate * sigmoid_g).astype(jnp.bfloat16)
    partial_value = lax.dot_general(
        gate_grad, gate_weight[0], contract, preferred_element_type=jnp.float32
    )
    partial_value = partial_value + lax.dot_general(
        up_grad, up_weight[0], contract, preferred_element_type=jnp.float32
    )
    partial_rounded = partial_value.astype(jnp.bfloat16)
    slot_grad = lax.psum_scatter(partial_rounded, "vocab", scatter_dimension=1, tiled=True).astype(
        jnp.float32
    )
    returned = lax.all_to_all(
        slot_grad.astype(jnp.bfloat16), "expert", split_axis=0, concat_axis=0, tiled=True
    ).astype(slot_grad.dtype)
    moe_grad = jnp.sum(returned[target].reshape(seq_len, top_k, d_slice), axis=1)
    resid = residual_stream.astype(jnp.float32)
    sum_squares = lax.psum(jnp.sum(resid * resid, axis=1), "vocab")
    inverse = lax.rsqrt(sum_squares / D + 1e-06)
    normed = resid * inverse[:, None]
    scaled = moe_grad * norm_gain[None, :]
    row_project = lax.psum(jnp.sum(scaled * normed, axis=1), "vocab") / D
    token_grad = (
        out_grad.astype(jnp.float32) + inverse[:, None] * (scaled - normed * row_project[:, None])
    ).astype(jnp.bfloat16)
    suffix_grad = lax.dynamic_slice_in_dim(token_grad, suffix_start[0], SUFFIX, 0)
    suffix_grad = lax.all_gather(suffix_grad, "vocab", axis=1, tiled=True)
    raw_scores = -lax.dot_general(
        lax.all_gather(suffix_grad, "expert", axis=0, tiled=True),
        embedding,
        contract,
        preferred_element_type=jnp.float32,
    )
    scores = jnp.where(allowed[None, :] > 0, raw_scores, jnp.float32(0.0))
    return (token_grad, scores)


def solution(mesh):
    placed = (
        P("expert", "vocab"),
        P("expert", "vocab"),
        P("vocab"),
        P("expert", None),
        P("expert", None),
        P("expert", None, "vocab"),
        P("expert", None, "vocab"),
        P("expert", None, "vocab"),
        P("expert", None, "vocab"),
        P("expert", "vocab", None),
        P(("expert", "vocab"), None),
        P(("expert", "vocab")),
        P("expert"),
    )
    return jax.shard_map(
        shards,
        mesh=mesh,
        in_specs=placed,
        out_specs=(P("expert", "vocab"), P(None, ("expert", "vocab"))),
        check_vma=False,
    )
```

profile of v0, /device:TPU:15, one launch (start us, length us, event | category | flops | bytes accessed | tf_op | source)
XLA Modules:
  0.0 500.4 jit_solution(15433524123861194605)
XLA Ops:
  7.2 0.0 copy-start
  7.2 0.0 all-gather.4.cloned.1.call-start
  7.2 0.9 copy.24
  8.2 0.1 eq.29
  8.3 0.1 eq.25
  8.3 0.7 broadcast_multiply_fusion
  9.0 4.5 reduce-window.6
  13.6 0.1 slice.10
  13.6 0.1 copy.26
  13.8 0.1 copy.27
  13.9 0.1 broadcast_add_fusion
  14.0 0.1 copy.23
  14.1 0.1 mul.95
  14.2 2.1 convert_element_type.50
  16.3 0.7 reduce_sum.50
  17.0 0.7 broadcast_divide_fusion
  17.7 0.1 copy.28
  17.8 0.1 mul.97
  18.0 10.3 %scatter_custom_fusion = bf16[1216,2048]{1,0:T(8,128)(2,1)} fusion(s32[1024]{0:T(1024)S(1)} %bitcast.64, f32[128,2048]{1,0:T(8,128)} %convert_element_type.50, f32[1024]{0:T(1024)S(1)} %mul.97, bf16[]{:T(256)} %constant.5.clone.1), kind=kCustom, calls=%fused_computation.14 | custom fusion | flops 4194304 | bytes 6033410 | tf_op jit(solution)/shard_map/scatter | solution.py:41
  28.3 7.3 %all_to_all.14 = bf16[16,76,2048]{2,1,0:T(8,128)(2,1)} reshape(bf16[1216,2048]{1,0:T(8,128)(2,1)} %scatter_custom_fusion) | data formatting | bytes 9961472 | tf_op jit(solution)/shard_map/all_to_all | solution.py:42
  35.6 120.4 %all_to_all.21 = bf16[16,76,2048]{2,1,0:T(8,128)(2,1)} all-to-all(bf16[16,76,2048]{2,1,0:T(8,128)(2,1)} %all_to_all.14), channel_id=1, replica_groups=mesh['expert'=16,'vocab'=2] {'expert'}, dimensions={0} | all-to-all | bytes 9961472 | tf_op jit(solution)/shard_map/all_to_all | solution.py:42
  156.0 7.4 %all_to_all.16 = bf16[1216,2048]{1,0:T(8,128)(2,1)} reshape(bf16[16,76,2048]{2,1,0:T(8,128)(2,1)} %all_to_all.21) | data formatting | bytes 9961472 | tf_op jit(solution)/shard_map/all_to_all | solution.py:42
  163.4 0.0 all-gather.4.cloned.1.call-update
  163.4 0.2 reduce-scatter.2.cloned.1.call-start
  163.6 23.8 %all-gather.4.cloned.1.call-done = bf16[1216,4096]{1,0:T(8,128)(2,1)} async-done(((bf16[1216,2048]{1,0:T(8,128)(2,1)}), bf16[1216,4096]{1,0:T(8,128)(2,1)}) %all-gather.4.cloned.1.call-update) | async-done | bytes 9961488 | tf_op jit(solution)/shard_map/all_gather | solution.py:43
  187.4 0.0 copy-start.6
  187.4 0.0 copy-start.7
  187.4 11.7 %fusion.4 = f32[1216,768]{1,0:T(8,128)S(1)} fusion(bf16[1216,4096]{1,0:T(8,128)(2,1)} %all-gather.4.cloned.1.call-done, bf16[1,768,4096]{2,1,0:T(8,128)(2,1)} %param.22), kind=kOutput, calls=%fused_computation.9 | convolution fusion | flops 7650410496 | bytes 19988480 | tf_op jit(solution)/shard_map/dot_general | solution.py:44
  199.1 0.0 copy-start.8
  199.1 1.8 copy-done.8
  200.9 0.0 copy-done.6
  200.9 0.0 copy-done.7
  200.9 14.5 %fusion.2 = f32[1216,4096]{1,0:T(8,128)} fusion(bf16[1,4096,768]{2,1,0:T(8,128)(2,1)} %param.20, f32[1216,768]{1,0:T(8,128)S(1)} %fusion.4, bf16[1,1216,768]{2,1,0:T(8,128)(2,1)S(1)} %copy-done.6, bf16[1,1216,768]{2,1,0:T(8,128)(2,1)S(1)} %copy-done.7), kind=kOutput, calls=%fused_computation.7 | convolution fusion | flops 7661617152 | bytes 33685504 | tf_op jit(solution)/shard_map/dot_general | solution.py:54
  215.4 17.2 %add_convert_fusion = bf16[1216,4096]{1,0:T(8,128)(2,1)} fusion(f32[1216,4096]{1,0:T(8,128)} %fusion.2, bf16[1,4096,768]{2,1,0:T(8,128)(2,1)} %param.21, f32[1216,768]{1,0:T(8,128)} %copy-done.8, bf16[1,1216,768]{2,1,0:T(8,128)(2,1)} %param.18), kind=kOutput, calls=%fused_computation.2 | convolution fusion | flops 7666909184 | bytes 41779200 | tf_op jit(solution)/shard_map/dot_general | solution.py:57
  232.6 0.0 reduce-scatter.2.cloned.1.call-update
  232.6 18.8 %reduce-scatter.2.cloned.1.call-done = bf16[1216,2048]{1,0:T(8,128)(2,1)} async-done(((bf16[1216,4096]{1,0:T(8,128)(2,1)}), bf16[1216,2048]{1,0:T(8,128)(2,1)}) %reduce-scatter.2.cloned.1.call-update) | async-done | bytes 4980752 | tf_op jit(solution)/shard_map/reduce_scatter | solution.py:61
  251.4 7.3 %all_to_all.17 = bf16[16,76,2048]{2,1,0:T(8,128)(2,1)} reshape(bf16[1216,2048]{1,0:T(8,128)(2,1)} %reduce-scatter.2.cloned.1.call-done) | data formatting | bytes 9961472 | tf_op jit(solution)/shard_map/all_to_all | solution.py:64
  258.7 6.4 %all-to-all-start.1 = ((bf16[16,76,2048]{2,1,0:T(8,128)(2,1)}), bf16[16,76,2048]{2,1,0:T(8,128)(2,1)}, u32[]{:S(2)}, u32[]{:S(2)}) async-start(bf16[16,76,2048]{2,1,0:T(8,128)(2,1)} %all_to_all.17), calls=%async_computation.2 | async-start | bytes 10485760 | tf_op jit(solution)/shard_map/all_to_all | solution.py:64
  265.1 0.0 all-gather.6.cloned.1.call-start
  265.8 1.2 fusion.35
  267.0 3.2 psum.14
  270.3 113.4 %all-to-all-done.1 = bf16[16,76,2048]{2,1,0:T(8,128)(2,1)} async-done(((bf16[16,76,2048]{2,1,0:T(8,128)(2,1)}), bf16[16,76,2048]{2,1,0:T(8,128)(2,1)}, u32[]{:S(2)}, u32[]{:S(2)}) %all-to-all-start.1) | async-done | bytes 4980768 | tf_op jit(solution)/shard_map/all_to_all | solution.py:64
  383.7 8.1 %reshape.79 = f32[1216,2048]{1,0:T(8,128)} reshape(bf16[16,76,2048]{2,1,0:T(8,128)(2,1)} %all-to-all-done.1) | data formatting | bytes 14942208 | tf_op jit(solution)/shard_map/convert_element_type | solution.py:66
  391.7 12.8 %gather_fusion = f32[1024,2048]{1,0:T(8,128)} fusion(f32[1216,2048]{1,0:T(8,128)} %reshape.79, s32[1024]{0:T(1024)S(1)} %broadcast_clamp_fusion), kind=kCustom, calls=%fused_computation | custom fusion | bytes 16781312 | tf_op jit(solution)/shard_map/gather | solution.py:67
  404.5 0.0 copy-start.2
  404.5 0.0 copy-start.4
  404.5 5.7 %bitcast_reduce_fusion = f32[128,2048]{1,0:T(8,128)S(1)} fusion(f32[1024,2048]{1,0:T(8,128)} %gather_fusion), kind=kLoop, calls=%fused_computation.3 | loop fusion | flops 1835008 | bytes 9437184 | tf_op jit(solution)/shard_map/reduce_sum | solution.py:67
  410.2 0.0 copy-start.1
  410.2 1.0 copy-done.1
  411.2 0.0 copy-done.2
  411.2 0.0 copy-done.4
  411.2 0.0 copy-start.5
  411.2 0.3 fusion.30
  411.5 3.5 psum.15
  415.0 1.9 fusion.34
  416.9 0.0 copy-start.3
  416.9 0.8 copy-done.3
  417.7 2.1 all_gather.10
  419.8 0.0 all-gather.6.cloned.1.call-update
  419.8 0.0 copy-done.5
  419.9 65.7 %all-gather.6.cloned.1.call-done = bf16[16,20,4096]{2,1,0:T(8,128)(2,1)} async-done(((bf16[1,20,4096]{2,1,0:T(8,128)(2,1)}), bf16[16,20,4096]{2,1,0:T(8,128)(2,1)}) %all-gather.6.cloned.1.call-update) | async-done | bytes 2621456 | tf_op jit(solution)/shard_map/all_gather | solution.py:80
  485.6 4.3 reshape.97
  489.8 0.0 copy-done
  489.9 4.1 fusion.29
  (10 shorter events, 0.1 us)
Async XLA Ops:
  7.2 482.7 %copy-start = (bf16[384,4096]{1,0:T(8,128)(2,1)S(1)}, bf16[384,4096]{1,0:T(8,128)(2,1)}, u32[]{:S(2)}) copy-start(bf16[384,4096]{1,0:T(8,128)(2,1)} %param.23) | copy-start | bytes 9437188
  7.2 180.2 %all-gather.4.cloned.1.call-start = ((), (), s32[]{:S(2)}) async-start(), calls=%async_computation.3 | async-start | bytes 14942208 | tf_op jit(solution)/shard_map/all_gather | solution.py:43
  163.4 88.0 %reduce-scatter.2.cloned.1.call-start = ((), (), s32[]{:S(2)}) async-start(), calls=%async_computation.4 | async-start | bytes 14942208 | tf_op jit(solution)/shard_map/reduce_scatter | solution.py:61
  187.4 13.5 %copy-start.6 = (bf16[1,1216,768]{2,1,0:T(8,128)(2,1)S(1)}, bf16[1,1216,768]{2,1,0:T(8,128)(2,1)}, u32[]{:S(2)}) copy-start(bf16[1,1216,768]{2,1,0:T(8,128)(2,1)} %param.19) | copy-start | bytes 5603332
  187.4 13.5 %copy-start.7 = (bf16[1,1216,768]{2,1,0:T(8,128)(2,1)S(1)}, bf16[1,1216,768]{2,1,0:T(8,128)(2,1)}, u32[]{:S(2)}) copy-start(bf16[1,1216,768]{2,1,0:T(8,128)(2,1)} %param.18) | copy-start | bytes 5603332
  199.1 1.8 copy-start.8
  258.7 125.0 %all-to-all-start.1 = ((bf16[16,76,2048]{2,1,0:T(8,128)(2,1)}), bf16[16,76,2048]{2,1,0:T(8,128)(2,1)}, u32[]{:S(2)}, u32[]{:S(2)}) async-start(bf16[16,76,2048]{2,1,0:T(8,128)(2,1)} %all_to_all.17), calls=%async_computation.2 | async-start | bytes 10485760 | tf_op jit(solution)/shard_map/all_to_all | solution.py:64
  265.1 220.5 %all-gather.6.cloned.1.call-start = ((), (), s32[]{:S(2)}) async-start(), calls=%async_computation.5 | async-start | bytes 3342336 | tf_op jit(solution)/shard_map/all_gather | solution.py:80
  404.5 6.7 %copy-start.2 = (bf16[128,2048]{1,0:T(8,128)(2,1)S(1)}, bf16[128,2048]{1,0:T(8,128)(2,1)}, u32[]{:S(2)}) copy-start(bf16[128,2048]{1,0:T(8,128)(2,1)} %param.14) | copy-start | bytes 1572868
  404.5 6.7 %copy-start.4 = (f32[2048]{0:T(1024)S(1)}, f32[2048]{0:T(1024)}, u32[]{:S(2)}) copy-start(f32[2048]{0:T(1024)} %param.15) | copy-start | bytes 24580
  410.2 1.0 copy-start.1
  411.2 8.6 %copy-start.5 = (s32[384]{0:T(512)S(1)}, s32[384]{0:T(512)}, u32[]{:S(2)}) copy-start(s32[384]{0:T(512)} %param.24) | copy-start | bytes 4612
  416.9 0.8 copy-start.3
Sparse Core Ops, SparseCore 0:
  163.5 23.8 all-gather.3
  232.7 18.5 reduce-scatter.1
  420.0 65.5 all-gather.5
where the time goes:
time: 505 us; the launch traced here: 500 us
  waiting for transfers between devices  222 us (44%)
  blocking collectives  129 us (26%)
  local copies, waits for them, and re-layouts  52.6 us (10%)
  matrix products  47.5 us (9%)
  other arithmetic  28.4 us (6%)
  between operations  14.5 us (3%)
  starting transfers between devices  6.7 us (1%)
    all_to_all x1, blocking collectives, shards(): lax.all_to_all(buffer, 'expert', split_axis=0, concat_axis=0, tiled=True)  120 us
    all_to_all x1, waiting for transfers between devices, shards(): lax.all_to_all(slot_grad.astype(jnp.bfloat16), 'expert', split_axis=0, co...  113 us
    all_gather x1, waiting for transfers between devices, shards(): lax.all_gather(suffix_grad, 'expert', axis=0, tiled=True)  65.7 us
    all_gather x1, waiting for transfers between devices, shards(): incoming = lax.all_gather(arrived, 'vocab', axis=1, tiled=True)  23.8 us
    reduce_scatter x1, waiting for transfers between devices, shards(): lax.psum_scatter(partial_rounded, 'vocab', scatter_dimension=1, tiled=True)  18.8 us
    dot_general x1, matrix products, shards(): lax.dot_general(up_grad, up_weight[0], contract, preferred_element_type=j...  17.2 us
    all_to_all x2, local copies, waits for them, and re-layouts, shards(): lax.all_to_all(buffer, 'expert', split_axis=0, concat_axis=0, tiled=True)  14.7 us
    dot_general x1, matrix products, shards(): lax.dot_general(gate_grad, gate_weight[0], contract, preferred_element_ty...  14.5 us
  transfers between devices with their start and end apart: 4, of which 4 were waited for; matrix products, arithmetic and copies ran while one was open for 0% of the time, Pallas kernels for 0%

commit v1 on v0

v1 whole, which is shorter than its diff:
```python
import functools

import jax
import jax.numpy as jnp
from jax import lax
from jax.experimental import pallas as pl
from jax.experimental.pallas import tpu as pltpu
from jax.sharding import PartitionSpec as P

D = 4096
SUFFIX = 20
MESH = pl.DeviceIdType.MESH


def dispatch_kernel(n, nv, src, out, here, send, recv, fsend, frecv):
    e, v = lax.axis_index("expert"), lax.axis_index("vocab")
    width = src.shape[2]

    def block_for(to):
        return src.at[to if src.shape[0] > 1 else 0]

    def place(row, col):
        return out.at[row, :, pl.ds(pl.multiple_of(col * width, 128), width)]

    local = pltpu.make_async_copy(block_for(e), place(e, v), here)
    local.start()

    def pass_on(j, i, block):
        row = lax.rem(e - j + n, n)
        return pltpu.make_async_remote_copy(
            src_ref=block,
            dst_ref=place(row, v),
            send_sem=fsend.at[j, i - 1],
            recv_sem=frecv.at[j, i - 1],
            device_id=(e, lax.rem(v + i, nv)),
            device_id_type=MESH,
        )

    def across(j):
        to = lax.rem(e + j, n)
        return pltpu.make_async_remote_copy(
            src_ref=block_for(to),
            dst_ref=place(e, v),
            send_sem=send.at[j],
            recv_sem=recv.at[j],
            device_id=(to, v),
            device_id_type=MESH,
        )

    for j in range(1, n):
        across(j).start()
    for i in range(1, nv):
        pass_on(0, i, block_for(e)).start()
    for j in range(1, n):
        across(j).wait_recv()
        for i in range(1, nv):
            pass_on(j, i, place(lax.rem(e - j + n, n), v)).start()
    for j in range(n):
        for i in range(1, nv):
            pass_on(j, i, block_for(e)).wait()
    for j in range(1, n):
        across(j).wait_send()
    local.wait()


def dispatch(blocks, n, nv):
    _, rows, width = blocks.shape
    return pl.pallas_call(
        functools.partial(dispatch_kernel, n, nv),
        out_shape=jax.ShapeDtypeStruct((n, rows, width * nv), blocks.dtype),
        in_specs=[pl.BlockSpec(memory_space=pl.ANY)],
        out_specs=pl.BlockSpec(memory_space=pl.ANY),
        scratch_shapes=[
            pltpu.SemaphoreType.DMA,
            pltpu.SemaphoreType.DMA((n,)),
            pltpu.SemaphoreType.DMA((n,)),
            pltpu.SemaphoreType.DMA((n, nv - 1)),
            pltpu.SemaphoreType.DMA((n, nv - 1)),
        ],
        compiler_params=pltpu.CompilerParams(has_side_effects=True),
    )(blocks)


def shards(
    out_grad,
    residual_stream,
    norm_gain,
    expert_ids,
    gate_scores,
    saved_gate,
    saved_up,
    gate_weight,
    up_weight,
    down_weight,
    embedding,
    allowed,
    suffix_start,
):
    n_expert = lax.axis_size("expert")
    seq_len, d_slice = out_grad.shape
    n_vocab = lax.axis_size("vocab")
    slot_count = saved_gate.shape[1]
    capacity = slot_count // n_expert
    padded = -(-capacity // 16) * 16
    contract = (((1,), (1,)), ((), ()))
    experts = jnp.arange(n_expert, dtype=jnp.int32)
    gate_share = gate_scores / jnp.sum(gate_scores, axis=1, keepdims=True)
    named = expert_ids[:, :, None] == experts
    chosen = jnp.any(named, axis=1)
    share = jnp.sum(jnp.where(named, gate_share[:, :, None], 0.0), axis=1)
    tokens = jnp.arange(seq_len, dtype=jnp.int32)
    earlier = (tokens[None, :] < tokens[:, None]).astype(jnp.bfloat16)
    position = jnp.dot(
        earlier, chosen.astype(jnp.bfloat16), preferred_element_type=jnp.float32
    ).astype(jnp.int32)
    position = jnp.where(chosen, position, -1).T
    holds = position[:, None, :] == jnp.arange(padded, dtype=jnp.int32)[None, :, None]
    share_of = jnp.sum(jnp.where(holds, share.T[:, None, :], 0.0), axis=2)
    pick = holds.astype(jnp.bfloat16).reshape(n_expert * padded, seq_len)
    taken = jnp.dot(pick, out_grad, preferred_element_type=jnp.float32)
    routed = (share_of.reshape(-1, 1) * taken).astype(jnp.bfloat16)
    incoming = dispatch(routed.reshape(n_expert, padded, d_slice), n_expert, n_vocab)
    incoming = incoming.reshape(n_expert * padded, d_slice * n_vocab)

    def widen(saved):
        wide = saved.reshape(n_expert, capacity, -1)
        wide = jnp.pad(wide, ((0, 0), (0, padded - capacity), (0, 0)))
        return wide.reshape(n_expert * padded, -1).astype(jnp.float32)

    act_grad = lax.dot_general(
        incoming, down_weight[0], contract, preferred_element_type=jnp.float32
    )
    pre_gate = widen(saved_gate[0])
    pre_up = widen(saved_up[0])
    sigmoid_g = jax.nn.sigmoid(pre_gate)
    gate_grad = (act_grad * pre_up * sigmoid_g * (1.0 + pre_gate * (1.0 - sigmoid_g))).astype(
        jnp.bfloat16
    )
    up_grad = (act_grad * pre_gate * sigmoid_g).astype(jnp.bfloat16)
    partial_value = lax.dot_general(
        gate_grad, gate_weight[0], contract, preferred_element_type=jnp.float32
    )
    partial_value = partial_value + lax.dot_general(
        up_grad, up_weight[0], contract, preferred_element_type=jnp.float32
    )
    partial_rounded = partial_value.astype(jnp.bfloat16)
    slot_grad = lax.psum_scatter(partial_rounded, "vocab", scatter_dimension=1, tiled=True)
    returned = lax.all_to_all(
        slot_grad.reshape(n_expert, padded, d_slice),
        "expert",
        split_axis=0,
        concat_axis=0,
        tiled=True,
    ).reshape(n_expert * padded, d_slice)
    moe_grad = lax.dot_general(
        pick, returned, (((0,), (0,)), ((), ())), preferred_element_type=jnp.float32
    )
    resid = residual_stream.astype(jnp.float32)
    scaled = moe_grad * norm_gain[None, :]
    sums = lax.psum(
        jnp.stack([jnp.sum(resid * resid, axis=1), jnp.sum(scaled * resid, axis=1)]), "vocab"
    )
    inverse = lax.rsqrt(sums[0] / D + 1e-06)
    normed = resid * inverse[:, None]
    row_project = inverse * (sums[1] / D)
    token_grad = (
        out_grad.astype(jnp.float32) + inverse[:, None] * (scaled - normed * row_project[:, None])
    ).astype(jnp.bfloat16)
    suffix_grad = lax.dynamic_slice_in_dim(token_grad, suffix_start[0], SUFFIX, 0)
    suffix_rows = -(-SUFFIX // 16) * 16
    suffix_grad = jnp.pad(suffix_grad, ((0, suffix_rows - SUFFIX), (0, 0)))
    suffix_grad = dispatch(suffix_grad[None], n_expert, n_vocab)[:, :SUFFIX]
    raw_scores = -lax.dot_general(
        suffix_grad.reshape(n_expert * SUFFIX, d_slice * n_vocab),
        embedding,
        contract,
        preferred_element_type=jnp.float32,
    )
    scores = jnp.where(allowed[None, :] > 0, raw_scores, jnp.float32(0.0))
    return (token_grad, scores)


def solution(mesh):
    placed = (
        P("expert", "vocab"),
        P("expert", "vocab"),
        P("vocab"),
        P("expert", None),
        P("expert", None),
        P("expert", None, "vocab"),
        P("expert", None, "vocab"),
        P("expert", None, "vocab"),
        P("expert", None, "vocab"),
        P("expert", "vocab", None),
        P(("expert", "vocab"), None),
        P(("expert", "vocab")),
        P("expert"),
    )
    return jax.shard_map(
        shards,
        mesh=mesh,
        in_specs=placed,
        out_specs=(P("expert", "vocab"), P(None, ("expert", "vocab"))),
        check_vma=False,
    )
```

time: 505 us -> 458 us (0.907)
  Pallas kernels: 0 us -> 211 us
  blocking collectives: 129 us -> 3.47 us
  waiting for transfers between devices: 222 us -> 135 us
  local copies, waits for them, and re-layouts: 52.6 us -> 21 us
  other arithmetic: 28.4 us -> 5.5 us
  matrix products: 47.5 us -> 59.3 us
    pallas_call x0 -> x2, Pallas kernels: none -> 211 us  [dispatch(): pl.pallas_call(functools.partial(dispatch_kernel, n, nv), out_shape=jax.S...]
    all_to_all x1 -> x0, blocking collectives: 120 us -> none  [shards(): lax.all_to_all(buffer, 'expert', split_axis=0, concat_axis=0, tiled=True)]
    all_gather x2 -> x0, waiting for transfers between devices: 89.5 us -> none  [the longest x1 65.7 us: shards(): lax.all_gather(suffix_grad, 'expert', axis=0, tiled=True)]
    all_to_all x3 -> x0, local copies, waits for them, and re-layouts: 22 us -> none  [the longest x2 14.7 us: shards(): lax.all_to_all(buffer, 'expert', split_axis=0, concat_axis=0, tiled=True)]
    gather x1 -> x0, local copies, waits for them, and re-layouts: 12.8 us -> none  [shards(): returned[target].reshape(seq_len, top_k, d_slice)]
    scatter x1 -> x0, other arithmetic: 10.3 us -> none  [shards(): jnp.zeros((slot_count, d_slice), jnp.bfloat16).at[target].set(routed)]
    dot_general x1 -> x4, matrix products: 4.06 us -> 13.7 us  [the longest x1 4.93 us: shards(): taken = jnp.dot(pick, out_grad, preferred_element_type=jnp.float32)]
    convert_element_type x1 -> x0, local copies, waits for them, and re-layouts: 8.07 us -> none  [shards(): returned = lax.all_to_all(slot_grad.astype(jnp.bfloat16), 'expert', split...]
  transfers between devices with their start and end apart: 4 -> 2, of which waited for: 4 -> 2; matrix products, arithmetic and copies ran while one was open for 0% -> 0% of each run, Pallas kernels for 0% -> 0%
where the time goes in v1:
time: 458 us; the launch traced here: 457 us
  Pallas kernels  211 us (46%)
  waiting for transfers between devices  135 us (29%)
  matrix products  59.3 us (13%)
  local copies, waits for them, and re-layouts  21 us (5%)
  between operations  14.8 us (3%)
  starting transfers between devices  6.57 us (1%)
  other arithmetic  5.5 us (1%)
    pallas_call x2, Pallas kernels, dispatch(): pl.pallas_call(functools.partial(dispatch_kernel, n, nv), out_shape=jax.S...  211 us
    all_to_all x1, waiting for transfers between devices, shards(): lax.all_to_all(slot_grad.reshape(n_expert, padded, d_slice), 'expert', sp...  118 us
    dot_general x1, matrix products, shards(): lax.dot_general(up_grad, up_weight[0], contract, preferred_element_type=j...  17.9 us
    reduce_scatter x1, waiting for transfers between devices, shards(): lax.psum_scatter(partial_rounded, 'vocab', scatter_dimension=1, tiled=True)  17.2 us
    dot_general x1, matrix products, shards(): lax.dot_general(gate_grad, gate_weight[0], contract, preferred_element_ty...  15.1 us
    dot_general x1, matrix products, shards(): lax.dot_general(incoming, down_weight[0], contract, preferred_element_typ...  12.6 us
  transfers between devices with their start and end apart: 2, of which 2 were waited for; matrix products, arithmetic and copies ran while one was open for 0% of the time, Pallas kernels for 0%

profile of v1, /device:TPU:15, one launch (start us, length us, event | category | flops | bytes accessed | tf_op | source)
XLA Modules:
  0.0 456.9 jit_solution(4350102517738187276)
XLA Ops:
  7.2 0.0 copy-start
  7.2 0.0 reduce-scatter.2.cloned.1.call-start
  7.2 0.9 fusion.29
  8.1 0.1 fusion.20
  8.2 0.1 eq.45
  8.3 0.7 reduce_sum.46
  9.0 0.7 broadcast_divide_fusion
  9.7 0.7 select_reduce_fusion.1
  10.4 0.2 bitcast_compare_fusion
  10.7 0.4 select_reduce_fusion
  11.0 0.1 mul.72
  11.1 4.9 %multiply_convert_fusion = bf16[1280,2048]{1,0:T(8,128)(2,1)} fusion(pred[1280,128]{1,0:T(32,128)(4,1)S(1)} %bitcast_compare_fusion, bf16[128,2048]{1,0:T(8,128)(2,1)} %param.13, f32[1280]{0:T(1024)S(1)} %mul.72), kind=kOutput, calls=%fused_computation.1 | convolution fusion | flops 676331520 | bytes 5936128 | tf_op jit(solution)/shard_map/dot_general | solution.py:120
  16.0 150.0 %shard_map.140 = bf16[16,80,4096]{2,1,0:T(8,128)(2,1)} custom-call(bf16[16,80,2048]{2,1,0:T(8,128)(2,1)} %bitcast.46), custom_call_target="tpu_custom_call" | custom-call | tf_op jit(solution)/shard_map/pallas_call | solution.py:68
  166.1 3.5 reshape_squeeze.7
  169.6 3.5 reshape_squeeze.6
  173.1 0.0 copy-start.1
  173.1 1.8 pad.12
  174.9 0.3 copy-done.1
  175.2 0.0 copy-start.2
  175.2 0.1 pad.11
  175.4 12.6 %fusion.3 = f32[1280,768]{1,0:T(8,128)S(1)} fusion(bf16[1280,4096]{1,0:T(8,128)(2,1)} %bitcast.47, bf16[1,768,4096]{2,1,0:T(8,128)(2,1)} %param.22), kind=kOutput, calls=%fused_computation.5 | convolution fusion | flops 8053063680 | bytes 20709376 | tf_op jit(solution)/shard_map/dot_general | solution.py:130
  188.0 0.0 copy-start.6
  188.0 0.0 copy-done.2
  188.0 1.8 copy-done.6
  189.9 15.1 %fusion.1 = f32[1280,4096]{1,0:T(8,128)} fusion(bf16[1,4096,768]{2,1,0:T(8,128)(2,1)} %param.20, bf16[1280,768]{1,0:T(8,128)(2,1)S(1)} %bitcast.49, f32[1280,768]{1,0:T(8,128)S(1)} %fusion.3, bf16[1280,768]{1,0:T(8,128)(2,1)S(1)} %bitcast.51), kind=kOutput, calls=%fused_computation.3 | convolution fusion | flops 8064860160 | bytes 35127296 | tf_op jit(solution)/shard_map/dot_general | solution.py:140
  204.9 17.9 %add_convert_fusion = bf16[1280,4096]{1,0:T(8,128)(2,1)} fusion(f32[1280,4096]{1,0:T(8,128)} %fusion.1, bf16[1,4096,768]{2,1,0:T(8,128)(2,1)} %param.21, f32[1280,768]{1,0:T(8,128)} %copy-done.6, bf16[1280,768]{1,0:T(8,128)(2,1)} %bitcast.50), kind=kOutput, calls=%fused_computation | convolution fusion | flops 8070430720 | bytes 43646976 | tf_op jit(solution)/shard_map/dot_general | solution.py:143
  222.9 0.0 reduce-scatter.2.cloned.1.call-update
  222.9 17.2 %reduce-scatter.2.cloned.1.call-done = bf16[1280,2048]{1,0:T(8,128)(2,1)} async-done(((bf16[1280,4096]{1,0:T(8,128)(2,1)}), bf16[1280,2048]{1,0:T(8,128)(2,1)}) %reduce-scatter.2.cloned.1.call-update) | async-done | bytes 5242896 | tf_op jit(solution)/shard_map/reduce_scatter | solution.py:147
  240.1 0.0 copy-start.5
  240.1 0.0 copy-start.4
  240.1 6.5 %all-to-all-start = ((bf16[16,80,2048]{2,1,0:T(8,128)(2,1)}), bf16[16,80,2048]{2,1,0:T(8,128)(2,1)}, u32[]{:S(2)}, u32[]{:S(2)}) async-start(bf16[16,80,2048]{2,1,0:T(8,128)(2,1)} %bitcast.48), calls=%async_computation.1 | async-start | bytes 10485760 | tf_op jit(solution)/shard_map/all_to_all | solution.py:148
  247.3 0.0 copy-done.5
  247.3 117.8 %all-to-all-done = bf16[16,80,2048]{2,1,0:T(8,128)(2,1)} async-done(((bf16[16,80,2048]{2,1,0:T(8,128)(2,1)}), bf16[16,80,2048]{2,1,0:T(8,128)(2,1)}, u32[]{:S(2)}, u32[]{:S(2)}) %all-to-all-start) | async-done | bytes 5242912 | tf_op jit(solution)/shard_map/all_to_all | solution.py:148
  365.1 0.0 copy-done.4
  365.1 4.6 %fusion.21 = (f32[128]{0:T(128)S(1)}, f32[128]{0:T(128)S(1)}, f32[128,2048]{1,0:T(8,128)}) fusion(bf16[128,2048]{1,0:T(8,128)(2,1)} %param.14, f32[2048]{0:T(1024)S(1)} %copy-done.4, bf16[16,80,2048]{2,1,0:T(8,128)(2,1)} %all-to-all-done, s32[16,128]{1,0:T(8,128)S(1)} %fusion.20), kind=kOutput, calls=%fused_computation.31 | convolution fusion | flops 672825088 | bytes 6833152 | tf_op jit(solution)/shard_map/dot_general | solution.py:155
  369.7 3.5 psum.7
  373.2 1.9 fusion.27
  375.1 0.0 copy-start.3
  375.1 0.8 copy-done.3
  376.0 0.7 pad_bitcast_fusion.src
  376.6 61.1 %shard_map.141 = bf16[16,32,4096]{2,1,0:T(8,128)(2,1)} custom-call(bf16[1,32,2048]{2,1,0:T(8,128)(2,1)} %pad_bitcast_fusion.src), custom_call_target="tpu_custom_call" | custom-call | tf_op jit(solution)/shard_map/pallas_call | solution.py:68
  437.8 3.9 slice.11
  441.7 4.3 reshape.62
  446.0 0.0 copy-done
  446.0 4.1 fusion.19
  (6 shorter events, 0.1 us)
Async XLA Ops:
  7.2 438.8 %copy-start = (bf16[384,4096]{1,0:T(8,128)(2,1)S(1)}, bf16[384,4096]{1,0:T(8,128)(2,1)}, u32[]{:S(2)}) copy-start(bf16[384,4096]{1,0:T(8,128)(2,1)} %param.23) | copy-start | bytes 9437188
  7.2 232.9 %reduce-scatter.2.cloned.1.call-start = ((), (), s32[]{:S(2)}) async-start(), calls=%async_computation.2 | async-start | bytes 15728640 | tf_op jit(solution)/shard_map/reduce_scatter | solution.py:147
  173.1 2.1 copy-start.1
  175.2 12.8 %copy-start.2 = (bf16[16,80,768]{2,1,0:T(8,128)(2,1)}, bf16[16,80,768]{2,1,0:T(8,128)(2,1)S(1)}, u32[]{:S(2)}) copy-start(bf16[16,80,768]{2,1,0:T(8,128)(2,1)S(1)} %pad.12) | copy-start | bytes 5898244
  188.0 1.9 copy-start.6
  240.1 7.2 %copy-start.5 = (s32[384]{0:T(512)S(1)}, s32[384]{0:T(512)}, u32[]{:S(2)}) copy-start(s32[384]{0:T(512)} %param.24) | copy-start | bytes 4612
  240.1 125.0 %copy-start.4 = (f32[2048]{0:T(1024)S(1)}, f32[2048]{0:T(1024)}, u32[]{:S(2)}) copy-start(f32[2048]{0:T(1024)} %param.15) | copy-start | bytes 24580
  240.1 125.0 %all-to-all-start = ((bf16[16,80,2048]{2,1,0:T(8,128)(2,1)}), bf16[16,80,2048]{2,1,0:T(8,128)(2,1)}, u32[]{:S(2)}, u32[]{:S(2)}) async-start(bf16[16,80,2048]{2,1,0:T(8,128)(2,1)} %bitcast.48), calls=%async_computation.1 | async-start | bytes 10485760 | tf_op jit(solution)/shard_map/all_to_all | solution.py:148
  375.1 0.8 copy-start.3
Sparse Core Ops, SparseCore 0:
  223.0 17.0 reduce-scatter.1
